TPU v7x, 32 devices: a whole 2x2x4 slice. The times are simulated.
32 devices in a mesh: dp: 8 (over z, x), mp: 4 (over y, core).
Axes of the slice: x: 2, y: 2, z: 4, core: 2. Of those that a mesh axis runs over, the one named last changes fastest.
Arguments:
- tokens: bfloat16 [1024, 4096], P('dp'), may hold values from -6 to 6
- cotangent: bfloat16 [1024, 4096], P('dp', 'mp'), may hold values from -6 to 6
- sketch: float32 [4096, 128], P('dp'), may hold values from -12 to 12
Outputs:
- precond: bfloat16 [4096, 4096], P('dp', 'mp')
- new_sketch: float32 [4096, 128], P('dp')
All inputs are finite; a program needn't handle non-finite values.
Results may differ from a plain program's by a relative error of at most 0.001.
Values sent between devices are 32-bit elements; how exact they have to be, the bound alone decides.
A program may use at most 64 MiB of HBM per device.

v0:
```python
import math
import jax
import jax.numpy as jnp
from jax import lax
from jax.sharding import PartitionSpec as P

DECAY_RATE = 0.9
RIDGE_FRAC = 0.0001


def product(left_mat, right_mat):
    return jnp.dot(left_mat, right_mat, precision=lax.Precision.HIGHEST)


def right_solve(values, lower_tri):
    return lax.linalg.triangular_solve(
        lower_tri, values, left_side=False, lower=True, transpose_a=True
    )


def left_solve(lower_tri, values, transpose):
    return lax.linalg.triangular_solve(
        lower_tri, values, left_side=True, lower=True, transpose_a=transpose
    )


def spd_solve(matrix, target):
    lower_tri = jnp.linalg.cholesky(matrix)
    return left_solve(lower_tri, left_solve(lower_tri, target, False), True)


def shards(tokens, cotangent, sketch):
    dp_count = lax.axis_size("dp")
    rank_size = sketch.shape[1]
    norm_scale = 1.0 / math.sqrt(tokens.shape[0] * dp_count)
    gradient = lax.psum_scatter(
        lax.dot_general(
            tokens, cotangent, (((0,), (0,)), ((), ())), preferred_element_type=jnp.float32
        )
        * norm_scale,
        "dp",
        scatter_dimension=0,
        tiled=True,
    )
    identity = jnp.eye(rank_size, dtype=jnp.float32)

    def covariance(sketch_proj, grad_proj):
        partial_cols = product(gradient, grad_proj)
        summed = lax.psum(partial_cols, "mp")
        return DECAY_RATE * product(sketch, sketch_proj) + summed

    sketch_proj, grad_proj = lax.psum(
        (product(sketch.T, sketch), product(gradient.T, sketch)), "dp"
    )
    applied = covariance(sketch_proj, grad_proj)
    gram_mat, sketch_image, grad_image = lax.psum(
        (product(applied.T, applied), product(sketch.T, applied), product(gradient.T, applied)),
        "dp",
    )
    previous_low = jnp.linalg.cholesky(gram_mat)
    previous = applied
    applied = covariance(
        right_solve(sketch_image, previous_low), right_solve(grad_image, previous_low)
    )
    cross_prev, self_image, image_grad = lax.psum(
        (product(previous.T, applied), product(applied.T, applied), product(applied.T, gradient)),
        "dp",
    )
    rayleigh = left_solve(previous_low, cross_prev, False)
    rayleigh = 0.5 * (rayleigh + rayleigh.T)
    mean_level = jnp.trace(rayleigh) / rank_size
    new_low = jnp.linalg.cholesky(rayleigh + RIDGE_FRAC * mean_level * identity)
    new_sketch = right_solve(applied, new_low)
    self_gram = right_solve(left_solve(new_low, self_image, False), new_low)
    cross_mat = left_solve(new_low, image_grad, False)
    inner_mat = mean_level * identity + self_gram
    precond = gradient - product(new_sketch, spd_solve(inner_mat, cross_mat))
    return (precond.astype(jnp.bfloat16), new_sketch)


def solution(mesh):
    in_specs = (P("dp", None), P("dp", "mp"), P("dp", None))
    out_specs = (P("dp", "mp"), P("dp", None))
    return jax.shard_map(shards, mesh=mesh, in_specs=in_specs, out_specs=out_specs, check_vma=False)
```

profile of v0, /device:TPU:0, one launch (start us, length us, event | category | flops | bytes accessed | tf_op | source)
XLA Modules:
  0.0 714.0 jit_solution(3880884214434900595)
XLA Ops:
  7.2 1.2 copy-done
  8.4 9.0 %convolution_multiply_fusion = f32[4096,1024]{1,0:T(8,128)} fusion(bf16[128,4096]{1,0:T(8,128)(2,1)S(1)} %copy-done, bf16[128,1024]{1,0:T(8,128)(2,1)} %param.11), kind=kOutput, calls=%fused_computation | convolution fusion | flops 1077936128 | bytes 18087936 | tf_op jit(solution)/shard_map/dot_general | solution.py:37
  17.5 0.9 copy-done.2
  18.4 1.2 fusion.33
  19.6 280.3 %reduce-scatter.2.cloned.1.call-done = f32[512,1024]{1,0:T(8,128)} async-done(((f32[4096,1024]{1,0:T(8,128)}), f32[512,1024]{1,0:T(8,128)}) %reduce-scatter.2.cloned.1.call-update) | async-done | bytes 2097168 | tf_op jit(solution)/shard_map/reduce_scatter | solution.py:36
  299.9 6.0 fusion.34
  305.9 72.5 %all-reduce.17.cloned.1.call-done = (f32[1024,128]{1,0:T(8,128)}, f32[128,128]{1,0:T(8,128)}) async-done(((f32[1024,128]{1,0:T(8,128)}, f32[128,128]{1,0:T(8,128)}), (f32[1024,128]{1,0:T(8,128)}, f32[128,128]{1,0:T(8,128)})) %all-reduce.17.cloned.1.call-update) | async-done | bytes 589840 | tf_op jit(solution)/shard_map/psum | solution.py:52
  378.4 4.1 fusion.35
  383.0 31.1 %all-reduce.9.cloned.1.call-done = f32[512,128]{0,1:T(8,128)} async-done(((f32[512,128]{0,1:T(8,128)}), f32[512,128]{0,1:T(8,128)}) %all-reduce.9.cloned.1.call-update) | async-done | bytes 262160 | tf_op jit(solution)/shard_map/psum | solution.py:49
  414.1 1.4 fusion.3
  415.5 1.0 convolution_bitcast_fusion.2
  416.5 1.0 fusion.36
  417.5 4.2 fusion.37
  421.8 74.2 %all-reduce.15.cloned.1.call-done = (f32[1024,128]{1,0:T(8,128)}, f32[128,128]{0,1:T(8,128)}, f32[128,128]{0,1:T(8,128)}) async-done(((f32[1024,128]{1,0:T(8,128)}, f32[128,128]{0,1:T(8,128)}, f32[128,128]{0,1:T(8,128)}), (f32[1024,128]{1,0:T(8,128)}, f32[128,128]{0,1:T(8,128)}, f32[128,128]{0,1:T(8,128)})) %all-reduce.15.cloned.1.call-update) | async-done | bytes 655376 | tf_op jit(solution)/shard_map/psum | solution.py:56
  496.0 0.9 copy.7
  496.9 0.9 fusion.27
  497.8 11.7 %cholesky.59 = f32[128,128]{1,0:T(8,128)S(1)} custom-call(f32[128,128]{1,0:T(8,128)S(1)} %fusion.27), custom_call_target="Cholesky" | custom-call | tf_op jit(solution)/shard_map/jit(cholesky)/cholesky | solution.py:60
  510.2 0.7 fusion.5
  510.8 9.8 %custom-call.26 = f32[1,128,128]{1,2,0:T(8,128)S(1)} custom-call(f32[1,128,128]{2,1,0:T(8,128)S(1)} %fusion.5), custom_call_target="InvertDiagBlocksLowerTriangular" | custom-call | tf_op jit(solution)/shard_map/triangular_solve/custom-call.0 | solution.py:16
  520.7 1.6 fusion.24
  522.3 3.0 fusion.38
  525.5 1.1 convolution_bitcast_fusion.1
  526.6 30.5 %all-reduce.11.cloned.1.call-done = f32[512,128]{0,1:T(8,128)} async-done(((f32[512,128]{0,1:T(8,128)}), f32[512,128]{0,1:T(8,128)}) %all-reduce.11.cloned.1.call-update) | async-done | bytes 262160 | tf_op jit(solution)/shard_map/psum | solution.py:49
  557.1 1.3 fusion.1
  558.5 2.0 fusion.39
  560.5 1.0 fusion.40
  561.5 2.1 fusion.41
  563.6 74.3 %all-reduce.13.cloned.1.call-done = (f32[128,128]{1,0:T(8,128)}, f32[128,1024]{1,0:T(8,128)}, f32[128,128]{1,0:T(8,128)}) async-done(((f32[128,128]{1,0:T(8,128)}, f32[128,1024]{1,0:T(8,128)}, f32[128,128]{1,0:T(8,128)}), (f32[128,128]{1,0:T(8,128)}, f32[128,1024]{1,0:T(8,128)}, f32[128,128]{1,0:T(8,128)})) %all-reduce.13.cloned.1.call-update) | async-done | bytes 655376 | tf_op jit(solution)/shard_map/psum | solution.py:65
  637.9 1.1 fusion.22
  640.4 0.9 fusion.32
  641.2 0.7 copy.10
  642.0 0.8 fusion.20
  642.8 0.7 copy.11
  643.5 12.5 %cholesky.70 = f32[128,128]{1,0:T(8,128)S(1)} custom-call(f32[128,128]{1,0:T(8,128)} %copy.11), custom_call_target="Cholesky" | custom-call | tf_op jit(solution)/shard_map/jit(cholesky)/cholesky | solution.py:72
  656.8 0.7 fusion.6
  657.4 9.8 %custom-call.21 = f32[1,128,128]{1,2,0:T(8,128)S(1)} custom-call(f32[1,128,128]{2,1,0:T(8,128)S(1)} %fusion.6), custom_call_target="InvertDiagBlocksLowerTriangular" | custom-call | tf_op jit(solution)/shard_map/triangular_solve | solution.py:16
  667.3 1.3 fusion.18
  668.5 1.8 fusion.15
  670.9 1.1 fusion.4
  672.0 0.7 copy.13
  672.7 1.5 fusion.12
  674.2 1.6 copy.14
  675.7 12.7 %cholesky.81 = f32[128,128]{1,0:T(8,128)S(1)} custom-call(f32[128,128]{1,0:T(8,128)} %copy.14), custom_call_target="Cholesky" | custom-call | tf_op jit(solution)/shard_map/jit(cholesky)/cholesky | solution.py:28
  688.5 0.7 compare_reduce_fusion
  689.2 1.3 fusion.7
  690.6 10.6 %custom-call.22 = f32[1,128,128]{1,2,0:T(8,128)S(1)} custom-call(f32[1,128,128]{2,1,0:T(8,128)} %fusion.7), custom_call_target="InvertDiagBlocksLowerTriangular" | custom-call | tf_op jit(solution)/shard_map/triangular_solve | solution.py:22
  701.2 1.7 fusion.13
  704.1 2.8 subtract_convert_fusion
  (37 shorter events, 4.3 us)
Async XLA Ops:
  7.2 1.2 copy-start
  7.2 292.7 %reduce-scatter.2.cloned.1.call-start = ((), (), s32[]{:S(2)}) async-start(), calls=%async_computation.1 | async-start | bytes 18874368 | tf_op jit(solution)/shard_map/reduce_scatter | solution.py:36
  17.4 0.9 copy-start.2
  17.5 361.0 %all-reduce.17.cloned.1.call-start = ((), (), s32[]{:S(2)}) async-start(), calls=%async_computation.6 | async-start | bytes 1179648 | tf_op jit(solution)/shard_map/psum | solution.py:52
  299.9 78.6 %copy-start.1 = (f32[512,1024]{1,0:T(8,128)S(1)}, f32[512,1024]{1,0:T(8,128)}, u32[]{:S(2)}) copy-start(f32[512,1024]{1,0:T(8,128)} %reduce-scatter.2.cloned.1.call-done) | copy-start | bytes 6291460
  305.9 108.2 %all-reduce.9.cloned.1.call-start = ((), (), s32[]{:S(2)}) async-start(), calls=%async_computation.2 | async-start | bytes 524288 | tf_op jit(solution)/shard_map/psum | solution.py:49
  378.4 35.7 %copy-start.8 = (f32[128,128]{1,0:T(8,128)S(1)}, f32[128,128]{1,0:T(8,128)}, u32[]{:S(2)}) copy-start(f32[128,128]{1,0:T(8,128)} %get-tuple-element.13) | copy-start | bytes 196612
  382.5 113.5 %all-reduce.15.cloned.1.call-start = ((), (), s32[]{:S(2)}) async-start(), calls=%async_computation.5 | async-start | bytes 1310720 | tf_op jit(solution)/shard_map/psum | solution.py:56
  415.5 2.0 copy-start.3
  421.8 135.4 %all-reduce.11.cloned.1.call-start = ((), (), s32[]{:S(2)}) async-start(), calls=%async_computation.3 | async-start | bytes 524288 | tf_op jit(solution)/shard_map/psum | solution.py:49
  525.3 112.7 %all-reduce.13.cloned.1.call-start = ((), (), s32[]{:S(2)}) async-start(), calls=%async_computation.4 | async-start | bytes 1310720 | tf_op jit(solution)/shard_map/psum | solution.py:65
  558.5 3.1 copy-start.4
  563.6 103.6 %copy-start.5 = (f32[512,128]{0,1:T(8,128)S(1)}, f32[512,128]{0,1:T(8,128)}, u32[]{:S(2)}) copy-start(f32[512,128]{0,1:T(8,128)} %copy-done.4) | copy-start | bytes 786436
  639.2 0.6 copy-start.7
  670.9 33.3 %copy-start.6 = (f32[512,128]{1,0:T(8,128)S(1)}, f32[512,128]{1,0:T(8,128)}, u32[]{:S(2)}) copy-start(f32[512,128]{1,0:T(8,128)} %fusion.18) | copy-start | bytes 786436
Sparse Core Ops, SparseCore 0:
  17.6 282.2 reduce-scatter.1
  306.0 72.3 all-reduce.16
  382.7 31.4 all-reduce.8
  421.9 74.0 all-reduce.14
  525.4 31.6 all-reduce.10
  563.7 74.1 all-reduce.12
where the time goes:
time: 721 us; the launch traced here: 714 us
  waiting for transfers between devices  563 us (78%)
  other arithmetic  76.7 us (11%)
  matrix products  51 us (7%)
  between operations  15.7 us (2%)
    reduce_scatter x1, waiting for transfers between devices, shards(): lax.psum_scatter(lax.dot_general(tokens, cotangent, (((0,), (0,)), ((), (...  280 us
    psum x1, waiting for transfers between devices, shards(): lax.psum((product(previous.T, applied), product(applied.T, applied), prod...  74.3 us
    psum x1, waiting for transfers between devices, shards(): lax.psum((product(applied.T, applied), product(sketch.T, applied), produc...  74.2 us
    psum x1, waiting for transfers between devices, shards(): lax.psum((product(sketch.T, sketch), product(gradient.T, sketch)), 'dp')  72.5 us
    psum x2, waiting for transfers between devices, covariance(): summed = lax.psum(partial_cols, 'mp')  61.6 us
    dot_general x13, matrix products, product(): return jnp.dot(left_mat, right_mat, precision=lax.Precision.HIGHEST)  31.1 us
    another operation x4, other arithmetic, right_solve(): lax.linalg.triangular_solve(lower_tri, values, left_side=False, lower=Tru...  20.9 us
  transfers between devices with their start and end apart: 6, of which 6 were waited for; matrix products, arithmetic and copies ran while one was open for 0% of the time, Pallas kernels for 0%

commit v1 on v0

--- a/solution.py
+++ b/solution.py
@@ -46,7 +46,7 @@
 
     def covariance(sketch_proj, grad_proj):
         partial_cols = product(gradient, grad_proj)
-        summed = lax.psum(partial_cols, "mp")
+        summed = jnp.sum(lax.all_gather(partial_cols, "mp"), axis=0)
         return DECAY_RATE * product(sketch, sketch_proj) + summed
 
     sketch_proj, grad_proj = lax.psum(

time: 721 us -> 697 us (0.967)
  waiting for transfers between devices: 563 us -> 532 us
    psum x2 -> x0, waiting for transfers between devices: 61.6 us -> none  [covariance(): summed = lax.psum(partial_cols, 'mp')]
    all_gather x0 -> x2, waiting for transfers between devices: none -> 30.4 us  [covariance(): summed = jnp.sum(lax.all_gather(partial_cols, 'mp'), axis=0)]
where the time goes in v1:
time: 697 us; the launch traced here: 689 us
  waiting for transfers between devices  532 us (76%)
  other arithmetic  81.3 us (12%)
  matrix products  50 us (7%)
  between operations  15.7 us (2%)
  local copies, waits for them, and re-layouts  9.79 us (1%)
    reduce_scatter x1, waiting for transfers between devices, shards(): lax.psum_scatter(lax.dot_general(tokens, cotangent, (((0,), (0,)), ((), (...  280 us
    psum x1, waiting for transfers between devices, shards(): lax.psum((product(previous.T, applied), product(applied.T, applied), prod...  74.3 us
    psum x1, waiting for transfers between devices, shards(): lax.psum((product(applied.T, applied), product(sketch.T, applied), produc...  74.2 us
    psum x1, waiting for transfers between devices, shards(): lax.psum((product(sketch.T, sketch), product(gradient.T, sketch)), 'dp')  72.5 us
    all_gather x2, waiting for transfers between devices, covariance(): summed = jnp.sum(lax.all_gather(partial_cols, 'mp'), axis=0)  30.4 us
    dot_general x13, matrix products, product(): return jnp.dot(left_mat, right_mat, precision=lax.Precision.HIGHEST)  30.1 us
    another operation x4, other arithmetic, right_solve(): lax.linalg.triangular_solve(lower_tri, values, left_side=False, lower=Tru...  22.4 us
  transfers between devices with their start and end apart: 6, of which 6 were waited for; matrix products, arithmetic and copies ran while one was open for 0% of the time, Pallas kernels for 0%

profile of v1, /device:TPU:0, one launch (start us, length us, event | category | flops | bytes accessed | tf_op | source)
XLA Modules:
  0.0 689.5 jit_solution(3854036273949587520)
XLA Ops:
  7.2 1.2 copy-done
  8.4 9.0 %convolution_multiply_fusion = f32[4096,1024]{1,0:T(8,128)} fusion(bf16[128,4096]{1,0:T(8,128)(2,1)S(1)} %copy-done, bf16[128,1024]{1,0:T(8,128)(2,1)} %param.11), kind=kOutput, calls=%fused_computation | convolution fusion | flops 1077936128 | bytes 18087936 | tf_op jit(solution)/shard_map/dot_general | solution.py:37
  17.5 0.9 copy-done.2
  18.4 1.2 fusion.33
  19.6 280.3 %reduce-scatter.2.cloned.1.call-done = f32[512,1024]{1,0:T(8,128)} async-done(((f32[4096,1024]{1,0:T(8,128)}), f32[512,1024]{1,0:T(8,128)}) %reduce-scatter.2.cloned.1.call-update) | async-done | bytes 2097168 | tf_op jit(solution)/shard_map/reduce_scatter | solution.py:36
  299.9 6.0 fusion.34
  305.9 72.5 %all-reduce.11.cloned.1.call-done = (f32[1024,128]{1,0:T(8,128)}, f32[128,128]{1,0:T(8,128)}) async-done(((f32[1024,128]{1,0:T(8,128)}, f32[128,128]{1,0:T(8,128)}), (f32[1024,128]{1,0:T(8,128)}, f32[128,128]{1,0:T(8,128)})) %all-reduce.11.cloned.1.call-update) | async-done | bytes 589840 | tf_op jit(solution)/shard_map/psum | solution.py:52
  378.4 3.6 fusion.35
  382.6 15.5 %all-gather.5.cloned.1.call-done = f32[2048,128]{1,0:T(8,128)} async-done(((f32[512,128]{1,0:T(8,128)}), f32[2048,128]{1,0:T(8,128)}) %all-gather.5.cloned.1.call-update) | async-done | bytes 1048592 | tf_op jit(solution)/shard_map/all_gather | solution.py:49
  398.0 2.0 reduce_sum.28
  400.0 1.8 copy.13
  401.8 1.4 fusion.3
  403.2 1.0 convolution_bitcast_fusion.2
  404.2 1.0 fusion.36
  405.2 4.2 fusion.37
  409.5 74.2 %all-reduce.9.cloned.1.call-done = (f32[1024,128]{1,0:T(8,128)}, f32[128,128]{0,1:T(8,128)}, f32[128,128]{0,1:T(8,128)}) async-done(((f32[1024,128]{1,0:T(8,128)}, f32[128,128]{0,1:T(8,128)}, f32[128,128]{0,1:T(8,128)}), (f32[1024,128]{1,0:T(8,128)}, f32[128,128]{0,1:T(8,128)}, f32[128,128]{0,1:T(8,128)})) %all-reduce.9.cloned.1.call-update) | async-done | bytes 655376 | tf_op jit(solution)/shard_map/psum | solution.py:56
  483.7 0.9 copy.15
  484.6 0.9 fusion.27
  485.5 11.7 %cholesky.59 = f32[128,128]{1,0:T(8,128)S(1)} custom-call(f32[128,128]{1,0:T(8,128)S(1)} %fusion.27), custom_call_target="Cholesky" | custom-call | tf_op jit(solution)/shard_map/jit(cholesky)/cholesky | solution.py:60
  497.9 1.3 fusion.5
  499.2 10.6 %custom-call.26 = f32[1,128,128]{1,2,0:T(8,128)S(1)} custom-call(f32[1,128,128]{2,1,0:T(8,128)} %fusion.5), custom_call_target="InvertDiagBlocksLowerTriangular" | custom-call | tf_op jit(solution)/shard_map/triangular_solve/custom-call.0 | solution.py:16
  509.8 1.6 fusion.24
  511.4 2.5 fusion.38
  514.2 1.1 convolution_bitcast_fusion.1
  515.3 14.9 %all-gather.7.cloned.1.call-done = f32[2048,128]{1,0:T(8,128)} async-done(((f32[512,128]{1,0:T(8,128)}), f32[2048,128]{1,0:T(8,128)}) %all-gather.7.cloned.1.call-update) | async-done | bytes 1048592 | tf_op jit(solution)/shard_map/all_gather | solution.py:49
  530.2 2.0 reduce_sum.29
  532.2 1.8 copy.16
  534.0 1.3 fusion.1
  535.4 2.0 fusion.39
  537.4 1.0 fusion.40
  538.4 2.1 fusion.41
  540.5 74.3 %all-reduce.7.cloned.1.call-done = (f32[128,128]{1,0:T(8,128)}, f32[128,1024]{1,0:T(8,128)}, f32[128,128]{1,0:T(8,128)}) async-done(((f32[128,128]{1,0:T(8,128)}, f32[128,1024]{1,0:T(8,128)}, f32[128,128]{1,0:T(8,128)}), (f32[128,128]{1,0:T(8,128)}, f32[128,1024]{1,0:T(8,128)}, f32[128,128]{1,0:T(8,128)})) %all-reduce.7.cloned.1.call-update) | async-done | bytes 655376 | tf_op jit(solution)/shard_map/psum | solution.py:65
  614.8 1.1 fusion.22
  617.3 0.9 fusion.32
  618.1 0.7 copy.18
  618.9 0.8 fusion.20
  619.8 11.7 %cholesky.70 = f32[128,128]{1,0:T(8,128)S(1)} custom-call(f32[128,128]{1,0:T(8,128)S(1)} %copy.19), custom_call_target="Cholesky" | custom-call | tf_op jit(solution)/shard_map/jit(cholesky)/cholesky | solution.py:72
  632.9 9.8 %custom-call.21 = f32[1,128,128]{1,2,0:T(8,128)S(1)} custom-call(f32[1,128,128]{2,1,0:T(8,128)S(1)} %fusion.6), custom_call_target="InvertDiagBlocksLowerTriangular" | custom-call | tf_op jit(solution)/shard_map/triangular_solve | solution.py:16
  642.7 1.3 fusion.18
  644.0 1.8 fusion.15
  646.3 1.1 fusion.4
  648.1 1.5 fusion.12
  649.6 1.6 copy.22
  651.2 12.7 %cholesky.81 = f32[128,128]{1,0:T(8,128)S(1)} custom-call(f32[128,128]{1,0:T(8,128)} %copy.22), custom_call_target="Cholesky" | custom-call | tf_op jit(solution)/shard_map/jit(cholesky)/cholesky | solution.py:28
  664.7 1.3 fusion.7
  666.0 10.6 %custom-call.22 = f32[1,128,128]{1,2,0:T(8,128)S(1)} custom-call(f32[1,128,128]{2,1,0:T(8,128)} %fusion.7), custom_call_target="InvertDiagBlocksLowerTriangular" | custom-call | tf_op jit(solution)/shard_map/triangular_solve | solution.py:22
  676.7 1.7 fusion.13
  679.6 2.8 subtract_convert_fusion
  (41 shorter events, 6.5 us)
Async XLA Ops:
  7.2 1.2 copy-start
  7.2 292.7 %reduce-scatter.2.cloned.1.call-start = ((), (), s32[]{:S(2)}) async-start(), calls=%async_computation.1 | async-start | bytes 18874368 | tf_op jit(solution)/shard_map/reduce_scatter | solution.py:36
  17.4 0.9 copy-start.2
  17.5 361.0 %all-reduce.11.cloned.1.call-start = ((), (), s32[]{:S(2)}) async-start(), calls=%async_computation.6 | async-start | bytes 1179648 | tf_op jit(solution)/shard_map/psum | solution.py:52
  299.9 78.6 %copy-start.1 = (f32[512,1024]{1,0:T(8,128)S(1)}, f32[512,1024]{1,0:T(8,128)}, u32[]{:S(2)}) copy-start(f32[512,1024]{1,0:T(8,128)} %reduce-scatter.2.cloned.1.call-done) | copy-start | bytes 6291460
  305.9 92.1 %all-gather.5.cloned.1.call-start = ((), (), s32[]{:S(2)}) async-start(), calls=%async_computation.2 | async-start | bytes 1310720 | tf_op jit(solution)/shard_map/all_gather | solution.py:49
  378.4 23.4 %copy-start.8 = (f32[128,128]{1,0:T(8,128)S(1)}, f32[128,128]{1,0:T(8,128)}, u32[]{:S(2)}) copy-start(f32[128,128]{1,0:T(8,128)} %get-tuple-element.13) | copy-start | bytes 196612
  382.0 101.7 %all-reduce.9.cloned.1.call-start = ((), (), s32[]{:S(2)}) async-start(), calls=%async_computation.5 | async-start | bytes 1310720 | tf_op jit(solution)/shard_map/psum | solution.py:56
  403.2 2.0 copy-start.3
  409.5 120.8 %all-gather.7.cloned.1.call-start = ((), (), s32[]{:S(2)}) async-start(), calls=%async_computation.3 | async-start | bytes 1310720 | tf_op jit(solution)/shard_map/all_gather | solution.py:49
  514.0 100.9 %all-reduce.7.cloned.1.call-start = ((), (), s32[]{:S(2)}) async-start(), calls=%async_computation.4 | async-start | bytes 1310720 | tf_op jit(solution)/shard_map/psum | solution.py:65
  535.4 3.1 copy-start.4
  540.5 102.2 %copy-start.5 = (f32[512,128]{0,1:T(8,128)S(1)}, f32[512,128]{0,1:T(8,128)}, u32[]{:S(2)}) copy-start(f32[512,128]{0,1:T(8,128)} %copy-done.4) | copy-start | bytes 786436
  616.1 0.6 copy-start.7
  646.3 33.3 %copy-start.6 = (f32[512,128]{1,0:T(8,128)S(1)}, f32[512,128]{1,0:T(8,128)}, u32[]{:S(2)}) copy-start(f32[512,128]{1,0:T(8,128)} %fusion.18) | copy-start | bytes 786436
Sparse Core Ops, SparseCore 0:
  17.6 282.2 reduce-scatter.1
  306.0 72.3 all-reduce.10
  382.2 15.8 all-gather.4
  409.6 74.0 all-reduce.8
  514.1 16.0 all-gather.6
  540.6 74.1 all-reduce.6
